TPU v7x, 128 devices: a whole 4x4x4 slice. The times are simulated.
128 devices in a mesh: pod: 1, dp: 16 (over z, y), sp: 8 (over x, core).
Axes of the slice: x: 4, y: 4, z: 4, core: 2. Of those that a mesh axis runs over, the one named last changes fastest.
Arguments:
- x: bfloat16 [48, 24, 128, 1152], P(('pod', 'dp'), 'sp')
- norm_gain: bfloat16 [2, 2, 1152], replicated
- norm_shift: bfloat16 [2, 2, 1152], replicated
- w_qkv: bfloat16 [2, 3, 1152, 16, 72], replicated
- w_out: bfloat16 [2, 16, 72, 1152], replicated
- w_up: bfloat16 [2, 1152, 4608], replicated
- w_down: bfloat16 [2, 4608, 1152], replicated
Outputs:
- output: bfloat16 [48, 24, 128, 1152], P(('pod', 'dp'), 'sp')
All inputs are finite; a program needn't handle non-finite values.
Results may differ from a plain program's by a relative error of at most 0.0161672.
Values are sent between devices in bfloat16 or wider.
A program may use at most 1 GiB of HBM per device.

v0:
```python
import functools

import jax
import jax.numpy as jnp
from jax import lax
from jax.experimental import pallas as pl
from jax.experimental.pallas import tpu as pltpu
from jax.sharding import PartitionSpec as P

LN_EPS = 1e-6
F32, BF16 = jnp.float32, jnp.bfloat16
UP_COLS = 512
LN_ROWS = 32
TANH_IN = 0.7978845608028654
TANH_CUBE = 0.044715


def gelu(u):
    inner = u * (TANH_IN + (TANH_IN * TANH_CUBE) * (u * u))
    half = 0.5 * u
    return half + half * jnp.tanh(inner)


def dot_nt(a, b):
    return lax.dot_general(a, b, (((1,), (1,)), ((), ())), preferred_element_type=F32)


def dot_nn(a, b):
    return jnp.dot(a, b, preferred_element_type=F32)


def ln_rows(tok, gain, shift):
    mean = jnp.mean(tok, axis=-1, keepdims=True)
    cen = tok - mean
    var = jnp.mean(cen * cen, axis=-1, keepdims=True)
    return (cen * lax.rsqrt(var + LN_EPS) * gain + shift).astype(BF16)


def kernel(dims, x_hbm, gain_ref, shift_ref, wqkv_hbm, wout_hbm, wup_hbm, wdown_hbm, y_hbm,
           xs, ns, rx, osend, orecv, wq, wo, wu, wd, nbuf, qkv, obuf, ubuf, gbuf, of32,
           xsem, wsem, ysem, send1, recv1, send2, recv2):
    nv, fr, npat, width, heads, hd, ff, n = dims
    rows = fr * npat
    pp = npat // n
    frames = fr * n
    me = lax.axis_index('sp')
    scale = hd ** -0.5
    barrier = pltpu.get_barrier_semaphore()

    def w_copy(block, which):
        if which < 3:
            return pltpu.make_async_copy(wqkv_hbm.at[block, which], wq.at[which], wsem.at[which])
        src, dst = [(wout_hbm, wo), (wup_hbm, wu), (wdown_hbm, wd)][which - 3]
        return pltpu.make_async_copy(src.at[block], dst, wsem.at[which])

    def x_copy(v):
        return pltpu.make_async_copy(x_hbm.at[v], xs.at[v], xsem.at[v])

    x_copy(0).start()
    for which in range(6):
        w_copy(0, which).start()
    for v in range(1, nv):
        x_copy(v).start()

    for step in range(1, n):
        peer = lax.rem(me + step, n)
        pl.semaphore_signal(barrier, inc=1, device_id={'sp': peer}, device_id_type=pl.DeviceIdType.MESH)

    def norm(v, block, which, write):
        gain = gain_ref[block, which:which + 1, :].astype(F32)
        shift = shift_ref[block, which:which + 1, :].astype(F32)
        for f in range(fr):
            for r in range(0, npat, LN_ROWS):
                write(f, r, ln_rows(xs[v, f, r:r + LN_ROWS, :].astype(F32), gain, shift))

    def to_nbuf(f, r, val):
        nbuf[f * npat + r:f * npat + r + LN_ROWS, :] = val

    def head_attn(qs, ks, vs, keep, write):
        tiles = width // 128
        lane = lax.broadcasted_iota(jnp.int32, (1, 128), 1)
        outs = [None] * tiles
        for h in range(heads):
            lo, hi = h * hd, (h + 1) * hd
            t0, t1 = lo // 128, (hi - 1) // 128
            q_parts = []
            for t in range(t0, t1 + 1):
                inside = (lane + t * 128 >= lo) & (lane + t * 128 < hi)
                part = qs(t)
                q_parts.append(jnp.where(inside, part, jnp.zeros_like(part)))
            qw = q_parts[0] if t0 == t1 else jnp.concatenate(q_parts, axis=1)
            s = dot_nt(qw, ks(t0, t1 + 1))
            s = keep(s)
            m = jnp.max(s, axis=-1, keepdims=True)
            e = jnp.exp((s - m) * scale)
            p = (e * (1.0 / jnp.sum(e, axis=-1, keepdims=True))).astype(BF16)
            o = dot_nn(p, vs(t0, t1 + 1))
            for t in range(t0, t1 + 1):
                part = o[:, (t - t0) * 128:(t - t0 + 1) * 128]
                if outs[t] is None:
                    outs[t] = part
                else:
                    outs[t] = jnp.where(lane + t * 128 >= lo, part, outs[t])
            for t in range(t0, t1 + 1):
                if (t + 1) * 128 <= hi:
                    write(t, outs[t])
                    outs[t] = None

    def tail(v, block, attn, first):
        @pl.when(first)
        def _():
            w_copy(block, 3).wait()
        a = dot_nn(attn, wo[...]).astype(BF16)
        for f in range(fr):
            h = xs[v, f].astype(F32) + a[f * npat:(f + 1) * npat].astype(F32)
            xs[v, f] = h.astype(BF16)
        norm(v, block, 1, to_nbuf)

        @pl.when(first)
        def _():
            w_copy(block, 4).wait()

        def up(c):
            cols = pl.ds(pl.multiple_of(c * UP_COLS, UP_COLS), UP_COLS)
            return dot_nn(nbuf[...], wu[:, cols]).astype(BF16)

        def act(c):
            cols = pl.ds(pl.multiple_of(c * UP_COLS, UP_COLS), UP_COLS)
            gbuf[:, cols] = gelu(ubuf[...].astype(F32)).astype(BF16)

        ubuf[...] = up(0)

        def up_step(c, carry):
            act(c - 1)
            ubuf[...] = up(c)
            return carry

        lax.fori_loop(1, ff // UP_COLS, up_step, 0)
        act(ff // UP_COLS - 1)

        @pl.when(first)
        def _():
            w_copy(block, 5).wait()

        def down(lo, cols):
            part = dot_nn(gbuf[...], wd[:, lo:lo + cols]).astype(BF16)
            for f in range(fr):
                h = xs[v, f, :, lo:lo + cols].astype(F32) + part[f * npat:(f + 1) * npat].astype(F32)
                xs[v, f, :, lo:lo + cols] = h.astype(BF16)

        for lo in range(0, width, 512):
            down(lo, min(512, width - lo))

    def send_copy(v, peer, stage):
        if stage == 1:
            return pltpu.make_async_remote_copy(
                src_ref=ns.at[v, :, pl.ds(pl.multiple_of(peer * pp, pp), pp), :],
                dst_ref=rx.at[v, pl.ds(me * fr, fr)],
                send_sem=send1.at[v, peer], recv_sem=recv1.at[v, me],
                device_id={'sp': peer}, device_id_type=pl.DeviceIdType.MESH)
        return pltpu.make_async_remote_copy(
            src_ref=osend.at[v, pl.ds(peer * fr, fr)],
            dst_ref=orecv.at[v, :, pl.ds(pl.multiple_of(me * pp, pp), pp), :],
            send_sem=send2.at[v, peer], recv_sem=recv2.at[v, me],
            device_id={'sp': peer}, device_id_type=pl.DeviceIdType.MESH)

    def recv_wait(v, peer, stage):
        if stage == 1:
            dst = rx.at[v, pl.ds(peer * fr, fr)]
            sem = recv1.at[v, peer]
        else:
            dst = orecv.at[v, :, pl.ds(pl.multiple_of(peer * pp, pp), pp), :]
            sem = recv2.at[v, peer]
        pltpu.make_async_copy(dst, dst, sem).wait()

    def each_peer(fn):
        for step in range(1, n):
            fn(lax.rem(me + step, n))

    def spatial(v, carry):
        x_copy(v).wait()
        norm(v, 0, 0, to_nbuf)

        def project(j, c):
            @pl.when(v == 0)
            def _():
                pltpu.make_async_copy(wqkv_hbm.at[0, j], wq.at[j], wsem.at[j]).wait()
            qkv[j] = dot_nt(nbuf[...], wq[j]).astype(BF16)
            return c

        lax.fori_loop(0, 3, project, 0)

        @pl.when(v == nv - 1)
        def _():
            for which in range(3):
                w_copy(1, which).start()

        def frame(f, c):
            rs = pl.ds(pl.multiple_of(f * npat, npat), npat)

            def write(t, val):
                obuf[rs, t * 128:(t + 1) * 128] = val.astype(BF16)

            head_attn(lambda t: qkv[0, rs, t * 128:(t + 1) * 128],
                      lambda a, b: qkv[1, rs, a * 128:b * 128],
                      lambda a, b: qkv[2, rs, a * 128:b * 128],
                      lambda s: s, write)
            return c

        lax.fori_loop(0, fr, frame, 0)
        tail(v, 0, obuf[...], v == 0)

        @pl.when(v == nv - 1)
        def _():
            for which in range(3, 6):
                w_copy(1, which).start()

        def to_ns(f, r, val):
            ns[v, f, r:r + LN_ROWS, :] = val

        norm(v, 1, 0, to_ns)

        @pl.when(v == 0)
        def _():
            pl.semaphore_wait(barrier, n - 1)

        rx[v, pl.ds(me * fr, fr)] = ns[v, :, pl.ds(pl.multiple_of(me * pp, pp), pp), :]
        each_peer(lambda peer: send_copy(v, peer, 1).start())
        return carry

    lax.fori_loop(0, nv, spatial, 0)

    half = 8
    groups = pp // half
    grows = frames * half

    def temporal(v, carry):
        each_peer(lambda peer: recv_wait(v, peer, 1))
        tok = rx[v].reshape(rows, width)

        def project(j, c):
            @pl.when(v == 0)
            def _():
                pltpu.make_async_copy(wqkv_hbm.at[1, j], wq.at[j], wsem.at[j]).wait()
            val = dot_nt(rx[v].reshape(rows, width), wq[j]).reshape(frames, groups, half, width)
            for g in range(groups):
                qkv[j, g * grows:(g + 1) * grows, :] = val[:, g].reshape(grows, width).astype(BF16)
            return c

        lax.fori_loop(0, 3, project, 0)
        sub = lax.broadcasted_iota(jnp.int32, (1, half, grows), 1)
        key = lax.broadcasted_iota(jnp.int32, (1, half, grows), 2)
        same = sub == lax.rem(key, half)

        def keep(s):
            return jnp.where(same, s.reshape(frames, half, grows), -jnp.inf).reshape(grows, grows)

        def group(g, c):
            rs = pl.ds(pl.multiple_of(g * grows, grows), grows)

            def write(t, val):
                of32[:, g, :, t * 128:(t + 1) * 128] = val.reshape(frames, half, 128)

            head_attn(lambda t: qkv[0, rs, t * 128:(t + 1) * 128],
                      lambda a, b: qkv[1, rs, a * 128:b * 128],
                      lambda a, b: qkv[2, rs, a * 128:b * 128],
                      keep, write)
            return c

        lax.fori_loop(0, groups, group, 0)
        for f in range(frames):
            osend[v, f] = of32[f].reshape(pp, width).astype(BF16)
        orecv[v, :, pl.ds(pl.multiple_of(me * pp, pp), pp), :] = osend[v, pl.ds(me * fr, fr)]
        each_peer(lambda peer: send_copy(v, peer, 2).start())
        return carry

    lax.fori_loop(0, nv, temporal, 0)

    def y_copy(v):
        return pltpu.make_async_copy(xs.at[v], y_hbm.at[v], ysem.at[v])

    def finish(v, carry):
        each_peer(lambda peer: recv_wait(v, peer, 2))
        tail(v, 1, orecv[v].reshape(rows, width), v == 0)
        y_copy(v).start()
        return carry

    lax.fori_loop(0, nv, finish, 0)
    for v in range(nv):
        y_copy(v).wait()
        each_peer(lambda peer: send_copy(v, peer, 1).wait_send())
        each_peer(lambda peer: send_copy(v, peer, 2).wait_send())


def solution(mesh):
    tok_spec = P(('pod', 'dp'), 'sp', None, None)
    n = mesh.shape['sp']

    def local_step(x, gain, shift, w_qkv, w_out, w_up, w_down):
        nv, fr, npat, width = x.shape
        heads, hd = w_qkv.shape[3:]
        ff = w_up.shape[2]
        rows = fr * npat
        wqkv_t = jnp.transpose(w_qkv, (0, 1, 3, 4, 2)).reshape(2, 3, heads * hd, width)
        wout_r = w_out.reshape(2, heads * hd, width)
        dims = (nv, fr, npat, width, heads, hd, ff, n)
        hbm = pl.BlockSpec(memory_space=pl.ANY)
        vmem = pl.BlockSpec(memory_space=pltpu.VMEM)
        pp, frames = npat // n, fr * n
        return pl.pallas_call(
            functools.partial(kernel, dims),
            out_shape=jax.ShapeDtypeStruct(x.shape, BF16),
            in_specs=[hbm, vmem, vmem, hbm, hbm, hbm, hbm],
            out_specs=hbm,
            scratch_shapes=[
                pltpu.VMEM((nv, fr, npat, width), BF16),
                pltpu.VMEM((nv, fr, npat, width), BF16),
                pltpu.VMEM((nv, frames, pp, width), BF16),
                pltpu.VMEM((nv, frames, pp, width), BF16),
                pltpu.VMEM((nv, fr, npat, width), BF16),
                pltpu.VMEM((3, heads * hd, width), BF16),
                pltpu.VMEM((heads * hd, width), BF16),
                pltpu.VMEM((width, ff), BF16),
                pltpu.VMEM((ff, width), BF16),
                pltpu.VMEM((rows, width), BF16),
                pltpu.VMEM((3, rows, heads * hd), BF16),
                pltpu.VMEM((rows, heads * hd), BF16),
                pltpu.VMEM((rows, UP_COLS), BF16),
                pltpu.VMEM((rows, ff), BF16),
                pltpu.VMEM((frames, pp // 8, 8, width), F32),
                pltpu.SemaphoreType.DMA((nv,)),
                pltpu.SemaphoreType.DMA((6,)),
                pltpu.SemaphoreType.DMA((nv,)),
                pltpu.SemaphoreType.DMA((nv, n)),
                pltpu.SemaphoreType.DMA((nv, n)),
                pltpu.SemaphoreType.DMA((nv, n)),
                pltpu.SemaphoreType.DMA((nv, n)),
            ],
            compiler_params=pltpu.CompilerParams(
                collective_id=0, has_side_effects=True, vmem_limit_bytes=67_000_000),
        )(x, gain, shift, wqkv_t, wout_r, w_up, w_down)

    return jax.shard_map(local_step, mesh=mesh, in_specs=(tok_spec, P(), P(), P(), P(), P(), P()), out_specs=tok_spec, check_vma=False)
```

profile of v0, /device:TPU:1, one launch (start us, length us, event | category | flops | bytes accessed | tf_op | source)
XLA Modules:
  0.0 164.7 jit_solution(6842080423023733582)
XLA Ops:
  0.0 161.2 %shard_map.73 = bf16[3,3,128,1152]{3,2,1,0:T(8,128)(2,1)} custom-call(bf16[3,3,128,1152]{3,2,1,0:T(8,128)(2,1)} %x_hbm.1, bf16[2,2,1152]{2,1,0:T(2,128)(2,1)} %gain_ref.1, bf16[2,2,1152]{2,1,0:T(2,128)(2,1)} %shift_ref.1, bf16[2,3,1152,1152]{3,2,1,0:T(8,128)(2,1)} %bitcast.4, bf16[2,1152,1152]{2,1,0:T(8,128)(2,1)} %bitcast.5, ...), custom_call_target="tpu_custom_call" | custom-call | tf_op jit(solution)/shard_map/pallas_call | solution.py:310
  161.2 3.5 %copy.9 = bf16[3,3,128,1152]{3,2,1,0:T(8,128)(2,1)} copy(bf16[3,3,128,1152]{3,2,1,0:T(8,128)(2,1)} %shard_map.73) | data formatting | bytes 5308416
where the time goes:
time: 165 us
  Pallas kernels  161 us (98%)
  local copies, waits for them, and re-layouts  3.47 us (2%)
    pallas_call x1, Pallas kernels, local_step(): pl.pallas_call(functools.partial(kernel, dims), out_shape=jax.ShapeDtypeS...  161 us
    unnamed x1, local copies, waits for them, and re-layouts  3.47 us

commit v1 on v0

--- a/solution.py
+++ b/solution.py
@@ -11,6 +11,8 @@
 F32, BF16 = jnp.float32, jnp.bfloat16
 UP_COLS = 512
 LN_ROWS = 32
+ATT_BUFS = 6
+QKV_SPLIT = 1792
 TANH_IN = 0.7978845608028654
 TANH_CUBE = 0.044715
 
@@ -37,7 +39,7 @@
 
 
 def kernel(dims, x_hbm, gain_ref, shift_ref, wqkv_hbm, wout_hbm, wup_hbm, wdown_hbm, y_hbm,
-           xs, ns, rx, osend, orecv, wq, wo, wu, wd, nbuf, qkv, obuf, ubuf, gbuf, of32,
+           xs, ns, rx, osend, orecv, wq, wo, wu, wd, nbuf, qkv, obuf, ubuf, gbuf, of32, sbuf, pbuf,
            xsem, wsem, ysem, send1, recv1, send2, recv2):
     nv, fr, npat, width, heads, hd, ff, n = dims
     rows = fr * npat
@@ -49,7 +51,7 @@
 
     def w_copy(block, which):
         if which < 3:
-            return pltpu.make_async_copy(wqkv_hbm.at[block, which], wq.at[which], wsem.at[which])
+            return pltpu.make_async_copy(wqkv_hbm.at[block, which], wq.at[which * width:(which + 1) * width], wsem.at[which])
         src, dst = [(wout_hbm, wo), (wup_hbm, wu), (wdown_hbm, wd)][which - 3]
         return pltpu.make_async_copy(src.at[block], dst, wsem.at[which])
 
@@ -76,35 +78,62 @@
     def to_nbuf(f, r, val):
         nbuf[f * npat + r:f * npat + r + LN_ROWS, :] = val
 
-    def head_attn(qs, ks, vs, keep, write):
+    def attend(units, masked):
         tiles = width // 128
         lane = lax.broadcasted_iota(jnp.int32, (1, 128), 1)
-        outs = [None] * tiles
-        for h in range(heads):
-            lo, hi = h * hd, (h + 1) * hd
-            t0, t1 = lo // 128, (hi - 1) // 128
-            q_parts = []
-            for t in range(t0, t1 + 1):
+        outs = {}
+        tops, sums = {}, {}
+
+        def span(h):
+            return h * hd, (h + 1) * hd, h * hd // 128, ((h + 1) * hd - 1) // 128 + 1
+
+        def buf(i):
+            return i % ATT_BUFS
+
+        def score(i):
+            base, nrow, h = units[i][:3]
+            lo, hi, t0, t1 = span(h)
+            parts = []
+            for t in range(t0, t1):
+                part = qkv[base:base + nrow, t * 128:(t + 1) * 128]
                 inside = (lane + t * 128 >= lo) & (lane + t * 128 < hi)
-                part = qs(t)
-                q_parts.append(jnp.where(inside, part, jnp.zeros_like(part)))
-            qw = q_parts[0] if t0 == t1 else jnp.concatenate(q_parts, axis=1)
-            s = dot_nt(qw, ks(t0, t1 + 1))
-            s = keep(s)
-            m = jnp.max(s, axis=-1, keepdims=True)
-            e = jnp.exp((s - m) * scale)
-            p = (e * (1.0 / jnp.sum(e, axis=-1, keepdims=True))).astype(BF16)
-            o = dot_nn(p, vs(t0, t1 + 1))
-            for t in range(t0, t1 + 1):
+                parts.append(jnp.where(inside, part, jnp.zeros_like(part)))
+            qw = parts[0] if len(parts) == 1 else jnp.concatenate(parts, axis=1)
+            keys = qkv[base:base + nrow, width + t0 * 128:width + t1 * 128]
+            sbuf[buf(i), :nrow, :nrow] = masked(dot_nt(qw, keys))
+
+        def top(i):
+            nrow = units[i][1]
+            tops[i] = jnp.max(sbuf[buf(i), :nrow, :nrow], axis=-1, keepdims=True)
+
+        def expo(i):
+            nrow = units[i][1]
+            e = jnp.exp((sbuf[buf(i), :nrow, :nrow] - tops.pop(i)) * scale)
+            sbuf[buf(i), :nrow, :nrow] = e
+            sums[i] = jnp.sum(e, axis=-1, keepdims=True)
+
+        def prob(i):
+            nrow = units[i][1]
+            pbuf[buf(i), :nrow, :nrow] = (sbuf[buf(i), :nrow, :nrow] * (1.0 / sums.pop(i))).astype(BF16)
+
+        def mix(i):
+            base, nrow, h, write = units[i]
+            lo, hi, t0, t1 = span(h)
+            o = dot_nn(pbuf[buf(i), :nrow, :nrow], qkv[base:base + nrow, 2 * width + t0 * 128:2 * width + t1 * 128])
+            for t in range(t0, t1):
                 part = o[:, (t - t0) * 128:(t - t0 + 1) * 128]
-                if outs[t] is None:
-                    outs[t] = part
+                if (base, t) in outs:
+                    part = jnp.where(lane + t * 128 >= lo, part, outs.pop((base, t)))
+                if (t + 1) * 128 <= hi:
+                    write(t, part)
                 else:
-                    outs[t] = jnp.where(lane + t * 128 >= lo, part, outs[t])
-            for t in range(t0, t1 + 1):
-                if (t + 1) * 128 <= hi:
-                    write(t, outs[t])
-                    outs[t] = None
+                    outs[(base, t)] = part
+
+        stages = ((score, 0), (top, 2), (expo, 3), (prob, 4), (mix, 5))
+        for i in range(len(units) + 5):
+            for fn, lag in reversed(stages):
+                if 0 <= i - lag < len(units):
+                    fn(i - lag)
 
     def tail(v, block, attn, first):
         @pl.when(first)
@@ -181,33 +210,23 @@
         x_copy(v).wait()
         norm(v, 0, 0, to_nbuf)
 
-        def project(j, c):
-            @pl.when(v == 0)
-            def _():
-                pltpu.make_async_copy(wqkv_hbm.at[0, j], wq.at[j], wsem.at[j]).wait()
-            qkv[j] = dot_nt(nbuf[...], wq[j]).astype(BF16)
-            return c
-
-        lax.fori_loop(0, 3, project, 0)
+        @pl.when(v == 0)
+        def _():
+            for which in range(3):
+                w_copy(0, which).wait()
+
+        for lo, hi in ((0, QKV_SPLIT), (QKV_SPLIT, 3 * width)):
+            qkv[:, lo:hi] = dot_nt(nbuf[...], wq[lo:hi, :]).astype(BF16)
 
         @pl.when(v == nv - 1)
         def _():
             for which in range(3):
                 w_copy(1, which).start()
 
-        def frame(f, c):
-            rs = pl.ds(pl.multiple_of(f * npat, npat), npat)
-
-            def write(t, val):
-                obuf[rs, t * 128:(t + 1) * 128] = val.astype(BF16)
-
-            head_attn(lambda t: qkv[0, rs, t * 128:(t + 1) * 128],
-                      lambda a, b: qkv[1, rs, a * 128:b * 128],
-                      lambda a, b: qkv[2, rs, a * 128:b * 128],
-                      lambda s: s, write)
-            return c
-
-        lax.fori_loop(0, fr, frame, 0)
+        def store(f, t, val):
+            obuf[f * npat:(f + 1) * npat, t * 128:(t + 1) * 128] = val.astype(BF16)
+
+        attend([(f * npat, npat, h, functools.partial(store, f)) for f in range(fr) for h in range(heads)], lambda s: s)
         tail(v, 0, obuf[...], v == 0)
 
         @pl.when(v == nv - 1)
@@ -236,18 +255,17 @@
 
     def temporal(v, carry):
         each_peer(lambda peer: recv_wait(v, peer, 1))
-        tok = rx[v].reshape(rows, width)
-
-        def project(j, c):
-            @pl.when(v == 0)
-            def _():
-                pltpu.make_async_copy(wqkv_hbm.at[1, j], wq.at[j], wsem.at[j]).wait()
-            val = dot_nt(rx[v].reshape(rows, width), wq[j]).reshape(frames, groups, half, width)
+
+        @pl.when(v == 0)
+        def _():
+            for which in range(3):
+                w_copy(1, which).wait()
+
+        for lo, hi in ((0, QKV_SPLIT), (QKV_SPLIT, 3 * width)):
+            val = dot_nt(rx[v].reshape(rows, width), wq[lo:hi, :]).reshape(frames, groups, half, hi - lo)
             for g in range(groups):
-                qkv[j, g * grows:(g + 1) * grows, :] = val[:, g].reshape(grows, width).astype(BF16)
-            return c
-
-        lax.fori_loop(0, 3, project, 0)
+                qkv[g * grows:(g + 1) * grows, lo:hi] = val[:, g].reshape(grows, hi - lo).astype(BF16)
+
         sub = lax.broadcasted_iota(jnp.int32, (1, half, grows), 1)
         key = lax.broadcasted_iota(jnp.int32, (1, half, grows), 2)
         same = sub == lax.rem(key, half)
@@ -255,19 +273,10 @@
         def keep(s):
             return jnp.where(same, s.reshape(frames, half, grows), -jnp.inf).reshape(grows, grows)
 
-        def group(g, c):
-            rs = pl.ds(pl.multiple_of(g * grows, grows), grows)
-
-            def write(t, val):
-                of32[:, g, :, t * 128:(t + 1) * 128] = val.reshape(frames, half, 128)
-
-            head_attn(lambda t: qkv[0, rs, t * 128:(t + 1) * 128],
-                      lambda a, b: qkv[1, rs, a * 128:b * 128],
-                      lambda a, b: qkv[2, rs, a * 128:b * 128],
-                      keep, write)
-            return c
-
-        lax.fori_loop(0, groups, group, 0)
+        def store(g, t, val):
+            of32[:, g, :, t * 128:(t + 1) * 128] = val.reshape(frames, half, 128)
+
+        attend([(g * grows, grows, h, functools.partial(store, g)) for g in range(groups) for h in range(heads)], keep)
         for f in range(frames):
             osend[v, f] = of32[f].reshape(pp, width).astype(BF16)
         orecv[v, :, pl.ds(pl.multiple_of(me * pp, pp), pp), :] = osend[v, pl.ds(me * fr, fr)]
@@ -318,16 +327,18 @@
                 pltpu.VMEM((nv, frames, pp, width), BF16),
                 pltpu.VMEM((nv, frames, pp, width), BF16),
                 pltpu.VMEM((nv, fr, npat, width), BF16),
-                pltpu.VMEM((3, heads * hd, width), BF16),
+                pltpu.VMEM((3 * heads * hd, width), BF16),
                 pltpu.VMEM((heads * hd, width), BF16),
                 pltpu.VMEM((width, ff), BF16),
                 pltpu.VMEM((ff, width), BF16),
                 pltpu.VMEM((rows, width), BF16),
-                pltpu.VMEM((3, rows, heads * hd), BF16),
+                pltpu.VMEM((rows, 3 * heads * hd), BF16),
                 pltpu.VMEM((rows, heads * hd), BF16),
                 pltpu.VMEM((rows, UP_COLS), BF16),
                 pltpu.VMEM((rows, ff), BF16),
                 pltpu.VMEM((frames, pp // 8, 8, width), F32),
+                pltpu.VMEM((ATT_BUFS, frames * 8, frames * 8), F32),
+                pltpu.VMEM((ATT_BUFS, frames * 8, frames * 8), BF16),
                 pltpu.SemaphoreType.DMA((nv,)),
                 pltpu.SemaphoreType.DMA((6,)),
                 pltpu.SemaphoreType.DMA((nv,)),

time: 165 us -> 144 us (0.87)
  Pallas kernels: 161 us -> 140 us
    pallas_call x1, Pallas kernels: 161 us -> 140 us  [local_step(): pl.pallas_call(functools.partial(kernel, dims), out_shape=jax.ShapeDtypeS...]
where the time goes in v1:
time: 144 us
  Pallas kernels  140 us (97%)
  local copies, waits for them, and re-layouts  3.47 us (2%)
    pallas_call x1, Pallas kernels, local_step(): pl.pallas_call(functools.partial(kernel, dims), out_shape=jax.ShapeDtypeS...  140 us
    unnamed x1, local copies, waits for them, and re-layouts  3.47 us

profile of v1, /device:TPU:1, one launch (start us, length us, event | category | flops | bytes accessed | tf_op | source)
XLA Modules:
  0.0 143.7 jit_solution(10678305361553378863)
XLA Ops:
  0.0 140.2 %shard_map.73 = bf16[3,3,128,1152]{3,2,1,0:T(8,128)(2,1)} custom-call(bf16[3,3,128,1152]{3,2,1,0:T(8,128)(2,1)} %x_hbm.1, bf16[2,2,1152]{2,1,0:T(2,128)(2,1)} %gain_ref.1, bf16[2,2,1152]{2,1,0:T(2,128)(2,1)} %shift_ref.1, bf16[2,3,1152,1152]{3,2,1,0:T(8,128)(2,1)} %bitcast.4, bf16[2,1152,1152]{2,1,0:T(8,128)(2,1)} %bitcast.5, ...), custom_call_target="tpu_custom_call" | custom-call | tf_op jit(solution)/shard_map/pallas_call | solution.py:319
  140.2 3.5 %copy.9 = bf16[3,3,128,1152]{3,2,1,0:T(8,128)(2,1)} copy(bf16[3,3,128,1152]{3,2,1,0:T(8,128)(2,1)} %shard_map.73) | data formatting | bytes 5308416

commit v2 on v1

v2 whole, which is shorter than its diff:
```python
import functools

import jax
import jax.numpy as jnp
from jax import lax
from jax.experimental import pallas as pl
from jax.experimental.pallas import tpu as pltpu
from jax.sharding import PartitionSpec as P

LN_EPS = 1e-6
F32, BF16 = jnp.float32, jnp.bfloat16
UP_COLS = 512
DOWN_COLS = 512
LN_ROWS = 32
ATT_BUFS = 6
TILES_A = 5
TANH_IN = 0.7978845608028654
TANH_CUBE = 0.044715


def gelu(u):
    inner = u * (TANH_IN + (TANH_IN * TANH_CUBE) * (u * u))
    half = 0.5 * u
    return half + half * jnp.tanh(inner)


def dot_nt(a, b):
    return lax.dot_general(a, b, (((1,), (1,)), ((), ())), preferred_element_type=F32)


def dot_tn(a, b):
    return lax.dot_general(a, b, (((0,), (0,)), ((), ())), preferred_element_type=F32)


def dot_nn(a, b):
    return jnp.dot(a, b, preferred_element_type=F32)


def ln_rows(tok, gain, shift):
    mean = jnp.mean(tok, axis=-1, keepdims=True)
    cen = tok - mean
    var = jnp.mean(cen * cen, axis=-1, keepdims=True)
    return (cen * lax.rsqrt(var + LN_EPS) * gain + shift).astype(BF16)


def kernel(dims, x_hbm, gain_ref, shift_ref, wqkv_hbm, wout_hbm, wup_hbm, wdown_hbm, y_hbm,
           xs, ns, rx, osend, orecv, wq, wo, wu, wd, nbuf, qkv, obuf, ubuf, gbuf, of32, sbuf, pbuf, hbuf,
           xsem, wsem, qsem, ysem, send1, recv1, send2, recv2):
    nv, fr, npat, width, heads, hd, ff, n = dims
    rows = fr * npat
    pp = npat // n
    frames = fr * n
    me = lax.axis_index('sp')
    scale = hd ** -0.5
    barrier = pltpu.get_barrier_semaphore()

    def w_copy(block, which):
        src, dst = [(wout_hbm, wo), (wup_hbm, wu), (wdown_hbm, wd)][which - 3]
        return pltpu.make_async_copy(src.at[block], dst, wsem.at[which])

    def x_copy(v):
        return pltpu.make_async_copy(x_hbm.at[v], xs.at[v], xsem.at[v])

    x_copy(0).start()

    for step in range(1, n):
        peer = lax.rem(me + step, n)
        pl.semaphore_signal(barrier, inc=1, device_id={'sp': peer}, device_id_type=pl.DeviceIdType.MESH)

    tiles = width // 128
    cols_a, cols_b = TILES_A * 128, width - TILES_A * 128
    all_a = 3 * cols_a
    piece = 2 * 128

    def col(which, t):
        if t < TILES_A:
            return which * cols_a + t * 128
        return all_a + which * cols_b + (t - TILES_A) * 128

    def wq_copies(block):
        for which in range(3):
            for part in range(2):
                first, size = (0, cols_a) if part == 0 else (cols_a, cols_b)
                dst = col(which, 0 if part == 0 else TILES_A)
                yield pltpu.make_async_copy(wqkv_hbm.at[block, which, first:first + size],
                                            wq.at[dst:dst + size], qsem.at[which, part])

    def norm(read, block, which, write, lo=0, hi=rows):
        gain = gain_ref[block, which:which + 1, :].astype(F32)
        shift = shift_ref[block, which:which + 1, :].astype(F32)
        for r in range(lo, hi, LN_ROWS):
            write(r, ln_rows(read(r).astype(F32), gain, shift))

    def read_xs(v):
        return lambda r: xs[v, r:r + LN_ROWS, :]

    def to_nbuf(r, val):
        nbuf[r:r + LN_ROWS, :] = val

    def pass_on(v):
        def to_ns(r, val):
            ns[v, r // npat, r % npat:r % npat + LN_ROWS, :] = val

        norm(read_xs(v), 1, 0, to_ns)

    def send_on(v):
        rx[v, pl.ds(me * fr, fr)] = ns[v, :, pl.ds(pl.multiple_of(me * pp, pp), pp), :]
        each_peer(lambda peer: send_copy(v, peer, 1).start())

    def attend(units, group, keep, fill):
        lane = lax.broadcasted_iota(jnp.int32, (1, 128), 1)
        outs = {}
        tops, sums = {}, {}

        def span(h):
            return h * hd, (h + 1) * hd, h * hd // 128, ((h + 1) * hd - 1) // 128 + 1

        def cols(base, nrow, which, t0, t1):
            lo, hi = col(which, t0), col(which, t1 - 1) + 128
            if hi - lo == (t1 - t0) * 128:
                return qkv[base:base + nrow, lo:hi]
            return jnp.concatenate([qkv[base:base + nrow, col(which, t):col(which, t) + 128] for t in range(t0, t1)], axis=1)

        def buf(i):
            return i % ATT_BUFS

        def score(i):
            base, nrow, h = units[i][:3]
            lo, hi, t0, t1 = span(h)
            parts = []
            for t in range(t0, t1):
                part = cols(base, nrow, 1, t, t + 1)
                inside = (lane + t * 128 >= lo) & (lane + t * 128 < hi)
                parts.append(jnp.where(inside, part, jnp.zeros_like(part)))
            kw = parts[0] if len(parts) == 1 else jnp.concatenate(parts, axis=1)
            asks = cols(base, nrow, 0, t0, t1)
            sbuf[buf(i), :nrow, :nrow] = dot_nt(kw, asks)

        def scores(i):
            nrow = units[i][1]
            return sbuf[buf(i), :nrow, :nrow].reshape(nrow // group, group, nrow)

        def top(i):
            tops[i] = jnp.max(scores(i), axis=0, keepdims=True)
            if keep is None:
                tops[i] = jnp.max(tops[i], axis=1, keepdims=True)

        def expo(i):
            nrow = units[i][1]
            e = jnp.exp((scores(i) - tops.pop(i)) * scale)
            sbuf[buf(i), :nrow, :nrow] = e.reshape(nrow, nrow)
            total = jnp.sum(e, axis=0, keepdims=True)
            if keep is None:
                total = jnp.sum(total, axis=1, keepdims=True)
            inv = 1.0 / total
            sums[i] = inv if keep is None else jnp.where(keep, inv, 0.0)

        def prob(i):
            nrow = units[i][1]
            pbuf[buf(i), :nrow, :nrow] = (scores(i) * sums.pop(i)).reshape(nrow, nrow).astype(BF16)

        def mix(i):
            base, nrow, h, write = units[i]
            lo, hi, t0, t1 = span(h)
            o = dot_tn(pbuf[buf(i), :nrow, :nrow], cols(base, nrow, 2, t0, t1))
            for t in range(t0, t1):
                part = o[:, (t - t0) * 128:(t - t0 + 1) * 128]
                if (base, t) in outs:
                    part = jnp.where(lane + t * 128 >= lo, part, outs.pop((base, t)))
                if (t + 1) * 128 <= hi:
                    write(t, part)
                else:
                    outs[(base, t)] = part

        stages = ((score, 0), (top, 2), (expo, 3), (prob, 4), (mix, 5))
        early = sum(1 for unit in units if span(unit[2])[3] <= TILES_A)
        places = [k * early // len(fill) for k in range(len(fill))]
        for i in range(len(units) + 5):
            for k, place in enumerate(places):
                if i == place:
                    fill[k]()
            for fn, lag in reversed(stages):
                if 0 <= i - lag < len(units):
                    fn(i - lag)

    def tail(v, stage):
        first = v == 0

        @pl.when(first)
        def _():
            for which in range(3, 6):
                w_copy(stage, which).wait()

        step = rows // 2

        def out(lo):
            a = dot_nn(obuf[lo:lo + step, :], wo[...]).astype(BF16)
            hbuf[lo:lo + step, :] = (xs[v, lo:lo + step, :].astype(F32) + a.astype(F32)).astype(BF16)

        def up(c, lo, size):
            ubuf[c % 2, lo:lo + size] = dot_nn(nbuf[lo:lo + size, :], wu[:, c * UP_COLS:(c + 1) * UP_COLS]).astype(BF16)

        def mid(lo):
            norm(lambda r: hbuf[r:r + LN_ROWS, :], stage, 1, to_nbuf, lo, lo + step)

        chunks = ff // UP_COLS

        def act(c):
            gbuf[:, c * UP_COLS:(c + 1) * UP_COLS] = gelu(ubuf[c % 2].astype(F32)).astype(BF16)

        out(0)
        mid(0)
        out(step)
        up(0, 0, step)
        mid(step)
        up(0, step, step)
        for c in range(1, chunks):
            act(c - 1)
            up(c, 0, rows)
        act(chunks - 1)
        norm(read_xs(jnp.minimum(v + 1, nv - 1)), 0, 0, to_nbuf)
        for lo in range(0, width, DOWN_COLS):
            hi = min(width, lo + DOWN_COLS)
            part = dot_nn(gbuf[...], wd[:, lo:hi]).astype(BF16)
            xs[v, :, lo:hi] = (hbuf[:, lo:hi].astype(F32) + part.astype(F32)).astype(BF16)

    def send_copy(v, peer, stage):
        if stage == 1:
            return pltpu.make_async_remote_copy(
                src_ref=ns.at[v, :, pl.ds(pl.multiple_of(peer * pp, pp), pp), :],
                dst_ref=rx.at[v, pl.ds(me * fr, fr)],
                send_sem=send1.at[v, peer], recv_sem=recv1.at[v, me],
                device_id={'sp': peer}, device_id_type=pl.DeviceIdType.MESH)
        return pltpu.make_async_remote_copy(
            src_ref=osend.at[v, pl.ds(peer * fr, fr)],
            dst_ref=orecv.at[v, :, pl.ds(pl.multiple_of(me * pp, pp), pp), :],
            send_sem=send2.at[v, peer], recv_sem=recv2.at[v, me],
            device_id={'sp': peer}, device_id_type=pl.DeviceIdType.MESH)

    def recv_wait(v, peer, stage):
        if stage == 1:
            dst = rx.at[v, pl.ds(peer * fr, fr)]
            sem = recv1.at[v, peer]
        else:
            dst = orecv.at[v, :, pl.ds(pl.multiple_of(peer * pp, pp), pp), :]
            sem = recv2.at[v, peer]
        pltpu.make_async_copy(dst, dst, sem).wait()

    def each_peer(fn):
        for step in range(1, n):
            fn(lax.rem(me + step, n))

    def spatial(v):
        @pl.when(v == 0)
        def _():
            for copy in wq_copies(0):
                copy.wait()
            for which in range(3, 6):
                w_copy(0, which).start()
            x_copy(1).start()

        prev = jnp.maximum(v - 1, 0)
        qkv[:, :all_a] = dot_nt(nbuf[...], wq[:all_a, :]).astype(BF16)
        pass_on(prev)

        @pl.when(v == 0)
        def _():
            pl.semaphore_wait(barrier, n - 1)

        @pl.when(v > 0)
        def _():
            send_on(prev)

        @pl.when(v < nv - 1)
        def _():
            x_copy(v + 1).wait()

        @pl.when(v < nv - 2)
        def _():
            x_copy(v + 2).start()

        def store(f, t, val):
            obuf[f * npat:(f + 1) * npat, t * 128:(t + 1) * 128] = val.astype(BF16)

        def project(lo):
            qkv[:, lo:lo + piece] = dot_nt(nbuf[...], wq[lo:lo + piece, :]).astype(BF16)

        early = [h for h in range(heads) if (h + 1) * hd <= cols_a]
        order = [(f, h) for f in range(fr) for h in early] + [(f, h) for f in range(fr) for h in range(len(early), heads)]
        attend([(f * npat, npat, h, functools.partial(store, f)) for f, h in order], 8, None,
               [functools.partial(project, lo) for lo in range(all_a, 3 * width, piece)])

        @pl.when(v == nv - 1)
        def _():
            for copy in wq_copies(1):
                copy.start()

    half = 8
    groups = pp // half
    grows = frames * half

    def temporal(v, carry):
        each_peer(lambda peer: recv_wait(v, peer, 1))

        @pl.when(v == 0)
        def _():
            for copy in wq_copies(1):
                copy.wait()

        def project(lo, hi):
            val = dot_nt(rx[v].reshape(rows, width), wq[lo:hi, :]).reshape(frames, groups, half, hi - lo)
            for g in range(groups):
                qkv[g * grows:(g + 1) * grows, lo:hi] = val[:, g].reshape(grows, hi - lo).astype(BF16)

        project(0, all_a)
        sub = lax.broadcasted_iota(jnp.int32, (1, half, grows), 1)
        key = lax.broadcasted_iota(jnp.int32, (1, half, grows), 2)
        same = sub == lax.rem(key, half)

        def store(g, t, val):
            of32[:, g, :, t * 128:(t + 1) * 128] = val.reshape(frames, half, 128)

        early = [h for h in range(heads) if (h + 1) * hd <= cols_a]
        order = [(g, h) for g in range(groups) for h in early] + [(g, h) for g in range(groups) for h in range(len(early), heads)]
        attend([(g * grows, grows, h, functools.partial(store, g)) for g, h in order], half, same,
               [functools.partial(project, lo, lo + piece) for lo in range(all_a, 3 * width, piece)])
        for f in range(frames):
            osend[v, f] = of32[f].reshape(pp, width).astype(BF16)
        orecv[v, :, pl.ds(pl.multiple_of(me * pp, pp), pp), :] = osend[v, pl.ds(me * fr, fr)]
        each_peer(lambda peer: send_copy(v, peer, 2).start())
        return carry

    def y_copy(v):
        return pltpu.make_async_copy(xs.at[v], y_hbm.at[v], ysem.at[v])

    for copy in wq_copies(0):
        copy.start()
    x_copy(0).wait()
    norm(read_xs(0), 0, 0, to_nbuf)

    def phase(i, carry):
        stage = jnp.where(i >= nv, 1, 0)
        v = i - stage * nv

        @pl.when(i < nv)
        def _():
            spatial(v)

        @pl.when(i == nv)
        def _():
            pass_on(nv - 1)
            send_on(nv - 1)
            lax.fori_loop(0, nv, temporal, 0)

        @pl.when(i >= nv)
        def _():
            each_peer(lambda peer: recv_wait(v, peer, 2))
            obuf[...] = orecv[v].reshape(rows, width)

        tail(v, stage)

        @pl.when(i == nv - 1)
        def _():
            for which in range(3, 6):
                w_copy(1, which).start()

        @pl.when(i >= nv)
        def _():
            y_copy(v).start()

        return carry

    lax.fori_loop(0, 2 * nv, phase, 0)
    for v in range(nv):
        y_copy(v).wait()
        each_peer(lambda peer: send_copy(v, peer, 1).wait_send())
        each_peer(lambda peer: send_copy(v, peer, 2).wait_send())


def solution(mesh):
    tok_spec = P(('pod', 'dp'), 'sp', None, None)
    n = mesh.shape['sp']

    def local_step(x, gain, shift, w_qkv, w_out, w_up, w_down):
        nv, fr, npat, width = x.shape
        heads, hd = w_qkv.shape[3:]
        ff = w_up.shape[2]
        rows = fr * npat
        wqkv_t = jnp.transpose(w_qkv, (0, 1, 3, 4, 2)).reshape(2, 3, heads * hd, width)
        wout_r = w_out.reshape(2, heads * hd, width)
        dims = (nv, fr, npat, width, heads, hd, ff, n)
        hbm = pl.BlockSpec(memory_space=pl.ANY)
        vmem = pl.BlockSpec(memory_space=pltpu.VMEM)
        pp, frames = npat // n, fr * n
        y = pl.pallas_call(
            functools.partial(kernel, dims),
            out_shape=jax.ShapeDtypeStruct((nv, rows, width), BF16),
            in_specs=[hbm, vmem, vmem, hbm, hbm, hbm, hbm],
            out_specs=hbm,
            scratch_shapes=[
                pltpu.VMEM((nv, rows, width), BF16),
                pltpu.VMEM((nv, fr, npat, width), BF16),
                pltpu.VMEM((nv, frames, pp, width), BF16),
                pltpu.VMEM((nv, frames, pp, width), BF16),
                pltpu.VMEM((nv, fr, npat, width), BF16),
                pltpu.VMEM((3 * heads * hd, width), BF16),
                pltpu.VMEM((heads * hd, width), BF16),
                pltpu.VMEM((width, ff), BF16),
                pltpu.VMEM((ff, width), BF16),
                pltpu.VMEM((rows, width), BF16),
                pltpu.VMEM((rows, 3 * heads * hd), BF16),
                pltpu.VMEM((rows, heads * hd), BF16),
                pltpu.VMEM((2, rows, UP_COLS), BF16),
                pltpu.VMEM((rows, ff), BF16),
                pltpu.VMEM((frames, pp // 8, 8, width), F32),
                pltpu.VMEM((ATT_BUFS, frames * 8, frames * 8), F32),
                pltpu.VMEM((ATT_BUFS, frames * 8, frames * 8), BF16),
                pltpu.VMEM((rows, width), BF16),
                pltpu.SemaphoreType.DMA((nv,)),
                pltpu.SemaphoreType.DMA((6,)),
                pltpu.SemaphoreType.DMA((3, 2)),
                pltpu.SemaphoreType.DMA((nv,)),
                pltpu.SemaphoreType.DMA((nv, n)),
                pltpu.SemaphoreType.DMA((nv, n)),
                pltpu.SemaphoreType.DMA((nv, n)),
                pltpu.SemaphoreType.DMA((nv, n)),
            ],
            compiler_params=pltpu.CompilerParams(
                collective_id=0, has_side_effects=True, vmem_limit_bytes=67_000_000),
        )(x.reshape(nv, rows, width), gain, shift, wqkv_t, wout_r, w_up, w_down)
        return y.reshape(x.shape)

    return jax.shard_map(local_step, mesh=mesh, in_specs=(tok_spec, P(), P(), P(), P(), P(), P()), out_specs=tok_spec, check_vma=False)
```

time: 144 us -> 126 us (0.88)
  Pallas kernels: 140 us -> 122 us
    pallas_call x1, Pallas kernels: 140 us -> 122 us  [local_step(): pl.pallas_call(functools.partial(kernel, dims), out_shape=jax.ShapeDtypeS...]
where the time goes in v2:
time: 126 us
  Pallas kernels  122 us (97%)
  local copies, waits for them, and re-layouts  3.47 us (3%)
    pallas_call x1, Pallas kernels, local_step(): pl.pallas_call(functools.partial(kernel, dims), out_shape=jax.ShapeDtypeS...  122 us
    unnamed x1, local copies, waits for them, and re-layouts  3.47 us

profile of v2, /device:TPU:1, one launch (start us, length us, event | category | flops | bytes accessed | tf_op | source)
XLA Modules:
  0.0 125.6 jit_solution(13459077610004107979)
XLA Ops:
  0.0 122.1 %shard_map.73 = bf16[3,384,1152]{2,1,0:T(8,128)(2,1)} custom-call(bf16[3,384,1152]{2,1,0:T(8,128)(2,1)} %bitcast.9, bf16[2,2,1152]{2,1,0:T(2,128)(2,1)} %gain_ref.1, bf16[2,2,1152]{2,1,0:T(2,128)(2,1)} %shift_ref.1, bf16[2,3,1152,1152]{3,2,1,0:T(8,128)(2,1)} %bitcast.6, bf16[2,1152,1152]{2,1,0:T(8,128)(2,1)} %bitcast.8, bf16[2,1152,4608]{2,1,0:T(8,128)(2,1)} %wup_hbm.1, ...), custom_call_target="tpu_custom_call" | custom-call | tf_op jit(solution)/shard_map/pallas_call | solution.py:395
  122.1 3.5 %copy.9 = bf16[3,3,128,1152]{3,2,1,0:T(8,128)(2,1)} copy(bf16[3,3,128,1152]{3,2,1,0:T(8,128)(2,1)} %bitcast.7) | data formatting | bytes 5308416
